TPU v7x, 32 devices: a whole 2x2x4 slice. The times are simulated.
32 devices in a mesh: energy: 16 (over z, y, core), cuts: 2 (over x).
Axes of the slice: x: 2, y: 2, z: 4, core: 2. Of those that a mesh axis runs over, the one named last changes fastest.
Arguments:
- green: bfloat16 [64, 2, 4, 128, 128], P('energy', 'cuts'), may hold values from -6 to 6
- offsets: int32 [4], replicated, may hold values from 1 to 2
- occupation: float32 [4], replicated, may hold values from 0.05 to 2
- coupling: bfloat16 [4, 3, 2, 128, 128], P(None, None, 'cuts'), may hold values from -0.25 to 0.25
Outputs:
- sigma: float32 [64, 2, 4, 128, 128], P('energy', 'cuts')
All inputs are finite; a program needn't handle non-finite values.
Results may differ from a plain program's by a relative error of at most 0.0041.
Values may be sent and summed in bfloat16 or wider, within the bound.
A program may use at most 64 MiB of HBM per device.

v0:
```python
import jax
import jax.numpy as jnp
from jax import lax
from jax.sharding import PartitionSpec as P

OFFMAX = 2


def padded(block, sides, width):
    for axis, dim in sides:
        count = lax.axis_size(axis)
        forward = [(i, i + 1) for i in range(count - 1)]
        backward = [(target, source) for source, target in forward]
        low = lax.ppermute(
            lax.slice_in_dim(block, block.shape[dim] - width, None, axis=dim), axis, forward
        )
        high = lax.ppermute(lax.slice_in_dim(block, 0, width, axis=dim), axis, backward)
        block = jnp.concatenate([low, block, high], axis=dim)
    return block


def self_energy(extended, offsets, occupation, coupling, energies, reach):
    slices = extended.shape[1] - 2
    orbitals = extended.shape[3]
    total = jnp.zeros((energies, slices, 4, orbitals, orbitals), jnp.float32)
    for branch in range(coupling.shape[0]):
        occupied = occupation[branch]
        lower = jnp.stack([occupied, occupied, occupied + 1.0, occupied + 1.0]).reshape(
            1, 1, 4, 1, 1
        )
        upper = jnp.stack([occupied + 1.0, occupied + 1.0, occupied, occupied]).reshape(
            1, 1, 4, 1, 1
        )
        below = lax.dynamic_slice_in_dim(extended, reach - offsets[branch], energies, 0)
        above = lax.dynamic_slice_in_dim(extended, reach + offsets[branch], energies, 0)
        mixed = (lower * below.astype(jnp.float32) + upper * above.astype(jnp.float32)).astype(
            jnp.bfloat16
        )
        for side in range(3):
            part = mixed[:, side : side + slices]
            block = coupling[branch, side]
            left = jnp.einsum(
                "sab,escbd->escad", block, part, preferred_element_type=jnp.float32
            ).astype(jnp.bfloat16)
            total = total + jnp.einsum(
                "escad,sfd->escaf", left, block, preferred_element_type=jnp.float32
            )
    return total


def body(green, offsets, occupation, coupling):
    energies = green.shape[0]
    reach = OFFMAX
    widened = padded(green, (("energy", 0),), reach)
    extended = padded(widened, (("cuts", 1),), 1)
    return self_energy(extended, offsets, occupation, coupling, energies, reach)


def solution(mesh):
    in_specs = (P("energy", "cuts", None, None, None), P(), P(), P(None, None, "cuts", None, None))
    out_specs = P("energy", "cuts", None, None, None)
    return jax.shard_map(body, mesh=mesh, in_specs=in_specs, out_specs=out_specs, check_vma=False)
```

profile of v0, /device:TPU:26, one launch (start us, length us, event | category | flops | bytes accessed | tf_op | source)
XLA Modules:
  0.0 77.3 jit_solution(7866700746824887830)
XLA Ops:
  0.0 1.3 %copy.5 = bf16[4,1,4,128,128]{3,4,2,0,1:T(8,128)(2,1)S(1)} copy(bf16[4,1,4,128,128]{4,3,2,1,0:T(8,128)(2,1)} %param.4) | data formatting | bytes 1048576 | tf_op args[0]
  1.3 0.0 copy-start.2
  1.3 0.0 copy-start.3
  1.4 1.9 %collective-permute-start = (bf16[2,1,4,128,128]{3,4,2,0,1:T(8,128)(2,1)S(1)}, bf16[2,1,4,128,128]{3,4,2,0,1:T(8,128)(2,1)S(1)}, u32[]{:S(2)}, u32[]{:S(2)}) collective-permute-start(bf16[2,1,4,128,128]{3,4,2,0,1:T(8,128)(2,1)S(1)} %get-tuple-element.9), channel_id=1, source_target_pairs={{0,2},{2,4},{4,6},{6,8},{8,10},{10,12},{12,14},{14,16},{16,18},{18... | collective-permute-start | bytes 786440 | tf_op jit(solution)/shard_map/ppermute | solution.py:14
  3.3 4.5 %collective-permute-start.1 = (bf16[2,1,4,128,128]{3,4,2,0,1:T(8,128)(2,1)S(1)}, bf16[2,1,4,128,128]{3,4,2,0,1:T(8,128)(2,1)S(1)}, u32[]{:S(2)}, u32[]{:S(2)}) collective-permute-start(bf16[2,1,4,128,128]{3,4,2,0,1:T(8,128)(2,1)S(1)} %get-tuple-element.10), channel_id=1, source_target_pairs={{2,0},{4,2},{6,4},{8,6},{10,8},{12,10},{14,12},{16,14},{18,16},{20... | collective-permute-start | bytes 786440 | tf_op jit(solution)/shard_map/ppermute | solution.py:17
  7.9 2.1 %collective-permute-done = bf16[2,1,4,128,128]{3,4,2,0,1:T(8,128)(2,1)S(1)} collective-permute-done((bf16[2,1,4,128,128]{3,4,2,0,1:T(8,128)(2,1)S(1)}, bf16[2,1,4,128,128]{3,4,2,0,1:T(8,128)(2,1)S(1)}, u32[]{:S(2)}, u32[]{:S(2)}) %collective-permute-start) | collective-permute-done | bytes 262176 | tf_op jit(solution)/shard_map/ppermute | solution.py:14
  10.0 1.8 %collective-permute-done.1 = bf16[2,1,4,128,128]{3,4,2,0,1:T(8,128)(2,1)S(1)} collective-permute-done((bf16[2,1,4,128,128]{3,4,2,0,1:T(8,128)(2,1)S(1)}, bf16[2,1,4,128,128]{3,4,2,0,1:T(8,128)(2,1)S(1)}, u32[]{:S(2)}, u32[]{:S(2)}) %collective-permute-start.1) | collective-permute-done | bytes 262176 | tf_op jit(solution)/shard_map/ppermute | solution.py:17
  11.7 0.1 pad_maximum_fusion.1
  11.9 2.5 %collective-permute-start.3 = (bf16[8,1,4,128,128]{3,4,2,0,1:T(8,128)(2,1)S(1)}, bf16[8,1,4,128,128]{3,4,2,0,1:T(8,128)(2,1)S(1)}, u32[]{:S(2)}, u32[]{:S(2)}) collective-permute-start(bf16[8,1,4,128,128]{3,4,2,0,1:T(8,128)(2,1)S(1)} %pad_maximum_fusion.1), channel_id=1, source_target_pairs={{1,0},{3,2},{5,4},{7,6},{9,8},{11,10},{13,12},{15,14},{17,16},{19,... | collective-permute-start | bytes 3145736 | tf_op jit(solution)/shard_map/ppermute | solution.py:17
  14.4 1.3 %collective-permute-start.2 = (bf16[8,1,4,128,128]{3,4,2,0,1:T(8,128)(2,1)S(1)}, bf16[8,1,4,128,128]{3,4,2,0,1:T(8,128)(2,1)}, u32[]{:S(2)}, u32[]{:S(2)}) collective-permute-start(bf16[8,1,4,128,128]{3,4,2,0,1:T(8,128)(2,1)S(1)} %pad_maximum_fusion.1), channel_id=1, source_target_pairs={{0,1},{2,3},{4,5},{6,7},{8,9},{10,11},{12,13},{14,15},{16,17},{18,... | collective-permute-start | bytes 3145736 | tf_op jit(solution)/shard_map/ppermute | solution.py:14
  15.7 0.7 fusion.64
  26.5 0.6 fusion.63
  29.6 0.7 pad_maximum_fusion.8
  30.3 0.6 pad_maximum_fusion.4
  30.9 0.6 pad_maximum_fusion.2
  31.6 0.7 pad_maximum_fusion.6
  32.3 5.5 %collective-permute-done.3 = bf16[8,1,4,128,128]{3,4,2,0,1:T(8,128)(2,1)S(1)} collective-permute-done((bf16[8,1,4,128,128]{3,4,2,0,1:T(8,128)(2,1)S(1)}, bf16[8,1,4,128,128]{3,4,2,0,1:T(8,128)(2,1)S(1)}, u32[]{:S(2)}, u32[]{:S(2)}) %collective-permute-start.3) | collective-permute-done | bytes 1048608 | tf_op jit(solution)/shard_map/ppermute | solution.py:17
  37.8 4.3 %collective-permute-done.2 = bf16[8,1,4,128,128]{3,4,2,0,1:T(8,128)(2,1)} collective-permute-done((bf16[8,1,4,128,128]{3,4,2,0,1:T(8,128)(2,1)S(1)}, bf16[8,1,4,128,128]{3,4,2,0,1:T(8,128)(2,1)}, u32[]{:S(2)}, u32[]{:S(2)}) %collective-permute-start.2) | collective-permute-done | bytes 1048608 | tf_op jit(solution)/shard_map/ppermute | solution.py:14
  42.1 1.4 %pad_maximum_fusion = bf16[8,3,4,128,128]{3,4,2,0,1:T(8,128)(2,1)S(1)} fusion(bf16[8,1,4,128,128]{3,4,2,0,1:T(8,128)(2,1)S(1)} %collective-permute-done.3, bf16[2,1,4,128,128]{3,4,2,0,1:T(8,128)(2,1)S(1)} %collective-permute-done.1, bf16[4,1,4,128,128]{3,4,2,0,1:T(8,128)(2,1)S(1)} %copy.5, bf16[2,1,4,128,128]{3,4,2,0,1:T(8,128)(2,1)S(1)} %collective-permute-done, ...), kind=kLoop, calls=%fused_computation | loop fusion | flops 6291456 | bytes 6291456 | tf_op jit(solution)/shard_map/concatenate | solution.py:18
  43.5 4.4 %add_convert_fusion = (bf16[4,3,4,128,128]{3,4,2,0,1:T(8,128)(2,1)S(1)}, bf16[4,3,4,128,128]{3,4,2,0,1:T(8,128)(2,1)}, bf16[4,3,4,128,128]{3,4,2,0,1:T(8,128)(2,1)}, bf16[4,3,4,128,128]{3,4,2,0,1:T(8,128)(2,1)S(1)}) fusion(bf16[8,3,4,128,128]{3,4,2,0,1:T(8,128)(2,1)S(1)} %pad_maximum_fusion, s32[]{:T(128)S(6)} %select_n.31, f32[4]{0:T(128)S(1)} %get-tuple-element.26, ...), kind=kLoop, calls=%fused_computation.1 | loop fusion | flops 18874368 | bytes 18874528 | tf_op jit(solution)/shard_map/convert_element_type | solution.py:36
  47.9 1.6 %fusion.13 = f32[4,4,128,128]{3,2,1,0:T(8,128)} fusion(bf16[4,3,4,128,128]{3,4,2,0,1:T(8,128)(2,1)S(1)} %get-tuple-element.8, bf16[4,3,1,128,128]{4,3,2,1,0:T(8,128)(2,1)S(1)} %copy-done.1), kind=kOutput, calls=%fused_computation.41 | convolution fusion | flops 134479872 | bytes 1638400 | tf_op jit(solution)/shard_map/escad,sfd->escaf/dot_general | solution.py:45
  49.5 2.8 %convolution_add_fusion.10 = f32[4,4,128,128]{3,2,1,0:T(8,128)} fusion(f32[4,4,128,128]{3,2,1,0:T(8,128)} %fusion.13, bf16[4,3,4,128,128]{3,4,2,0,1:T(8,128)(2,1)S(1)} %get-tuple-element.8, bf16[4,3,1,128,128]{4,3,2,1,0:T(8,128)(2,1)S(1)} %copy-done.1), kind=kOutput, calls=%fused_computation.16 | convolution fusion | flops 134742016 | bytes 2686976 | tf_op jit(solution)/shard_map/escad,sfd->escaf/dot_general | solution.py:45
  52.3 2.8 %convolution_add_fusion.9 = f32[4,4,128,128]{3,2,1,0:T(8,128)} fusion(f32[4,4,128,128]{3,2,1,0:T(8,128)} %convolution_add_fusion.10, bf16[4,3,4,128,128]{3,4,2,0,1:T(8,128)(2,1)S(1)} %get-tuple-element.8, bf16[4,3,1,128,128]{4,3,2,1,0:T(8,128)(2,1)S(1)} %copy-done.1), kind=kOutput, calls=%fused_computation.15 | convolution fusion | flops 134742016 | bytes 2686976 | tf_op jit(solution)/shard_map/escad,sfd->escaf/dot_general | solution.py:45
  55.0 2.0 %convolution_add_fusion.8 = f32[4,4,128,128]{3,2,1,0:T(8,128)S(1)} fusion(f32[4,4,128,128]{3,2,1,0:T(8,128)} %convolution_add_fusion.9, bf16[4,3,4,128,128]{3,4,2,0,1:T(8,128)(2,1)} %get-tuple-element.6, bf16[4,3,1,128,128]{4,3,2,1,0:T(8,128)(2,1)S(1)} %copy-done.1), kind=kOutput, calls=%fused_computation.14 | convolution fusion | flops 134742016 | bytes 2686976 | tf_op jit(solution)/shard_map/escad,sfd->escaf/dot_general | solution.py:45
  57.0 2.6 %convolution_add_fusion.7 = f32[4,4,128,128]{3,2,1,0:T(8,128)} fusion(f32[4,4,128,128]{3,2,1,0:T(8,128)S(1)} %convolution_add_fusion.8, bf16[4,3,4,128,128]{3,4,2,0,1:T(8,128)(2,1)} %get-tuple-element.6, bf16[4,3,1,128,128]{4,3,2,1,0:T(8,128)(2,1)S(1)} %copy-done.1), kind=kOutput, calls=%fused_computation.13 | convolution fusion | flops 134742016 | bytes 2686976 | tf_op jit(solution)/shard_map/escad,sfd->escaf/dot_general | solution.py:45
  59.6 3.1 %convolution_add_fusion.6 = f32[4,4,128,128]{3,2,1,0:T(8,128)} fusion(f32[4,4,128,128]{3,2,1,0:T(8,128)} %convolution_add_fusion.7, bf16[4,3,4,128,128]{3,4,2,0,1:T(8,128)(2,1)} %get-tuple-element.6, bf16[4,3,1,128,128]{4,3,2,1,0:T(8,128)(2,1)S(1)} %copy-done.1), kind=kOutput, calls=%fused_computation.12 | convolution fusion | flops 134742016 | bytes 2686976 | tf_op jit(solution)/shard_map/escad,sfd->escaf/dot_general | solution.py:45
  62.7 2.8 %convolution_add_fusion.5 = f32[4,4,128,128]{3,2,1,0:T(8,128)} fusion(f32[4,4,128,128]{3,2,1,0:T(8,128)} %convolution_add_fusion.6, bf16[4,3,4,128,128]{3,4,2,0,1:T(8,128)(2,1)S(1)} %copy-done, bf16[4,3,1,128,128]{4,3,2,1,0:T(8,128)(2,1)S(1)} %copy-done.1), kind=kOutput, calls=%fused_computation.11 | convolution fusion | flops 134742016 | bytes 2686976 | tf_op jit(solution)/shard_map/escad,sfd->escaf/dot_general | solution.py:45
  65.5 2.8 %convolution_add_fusion.4 = f32[4,4,128,128]{3,2,1,0:T(8,128)} fusion(f32[4,4,128,128]{3,2,1,0:T(8,128)} %convolution_add_fusion.5, bf16[4,3,4,128,128]{3,4,2,0,1:T(8,128)(2,1)S(1)} %copy-done, bf16[4,3,1,128,128]{4,3,2,1,0:T(8,128)(2,1)S(1)} %copy-done.1), kind=kOutput, calls=%fused_computation.10 | convolution fusion | flops 134742016 | bytes 2686976 | tf_op jit(solution)/shard_map/escad,sfd->escaf/dot_general | solution.py:45
  68.3 2.8 %convolution_add_fusion.3 = f32[4,4,128,128]{3,2,1,0:T(8,128)} fusion(f32[4,4,128,128]{3,2,1,0:T(8,128)} %convolution_add_fusion.4, bf16[4,3,4,128,128]{3,4,2,0,1:T(8,128)(2,1)S(1)} %copy-done, bf16[4,3,1,128,128]{4,3,2,1,0:T(8,128)(2,1)S(1)} %copy-done.1), kind=kOutput, calls=%fused_computation.9 | convolution fusion | flops 134742016 | bytes 2686976 | tf_op jit(solution)/shard_map/escad,sfd->escaf/dot_general | solution.py:45
  71.1 2.8 %convolution_add_fusion.2 = f32[4,4,128,128]{3,2,1,0:T(8,128)} fusion(f32[4,4,128,128]{3,2,1,0:T(8,128)} %convolution_add_fusion.3, bf16[4,3,4,128,128]{3,4,2,0,1:T(8,128)(2,1)S(1)} %get-tuple-element.5, bf16[4,3,1,128,128]{4,3,2,1,0:T(8,128)(2,1)S(1)} %copy-done.1), kind=kOutput, calls=%fused_computation.8 | convolution fusion | flops 134742016 | bytes 2686976 | tf_op jit(solution)/shard_map/escad,sfd->escaf/dot_general | solution.py:45
  73.9 1.8 %convolution_add_fusion.1 = f32[4,4,128,128]{3,2,1,0:T(8,128)S(1)} fusion(f32[4,4,128,128]{3,2,1,0:T(8,128)} %convolution_add_fusion.2, bf16[4,3,4,128,128]{3,4,2,0,1:T(8,128)(2,1)S(1)} %get-tuple-element.5, bf16[4,3,1,128,128]{4,3,2,1,0:T(8,128)(2,1)S(1)} %copy-done.1), kind=kOutput, calls=%fused_computation.7 | convolution fusion | flops 134742016 | bytes 2686976 | tf_op jit(solution)/shard_map/escad,sfd->escaf/dot_general | solution.py:45
  75.7 1.6 %fusion = f32[4,1,4,128,128]{4,3,2,1,0:T(8,128)} fusion(f32[4,4,128,128]{3,2,1,0:T(8,128)S(1)} %convolution_add_fusion.1, bf16[4,3,4,128,128]{3,4,2,0,1:T(8,128)(2,1)S(1)} %get-tuple-element.5, bf16[4,3,1,128,128]{4,3,2,1,0:T(8,128)(2,1)S(1)} %copy-done.1), kind=kOutput, calls=%fused_computation.6 | convolution fusion | flops 134742016 | bytes 2686976 | tf_op jit(solution)/shard_map/escad,sfd->escaf/dot_general | solution.py:45
  (7 shorter events, 0.1 us)
Async XLA Ops:
  1.3 14.4 %copy-start.2 = (s32[4]{0:T(128)S(1)}, s32[4]{0:T(128)}, u32[]{:S(2)}) copy-start(s32[4]{0:T(128)} %param.5) | copy-start | bytes 52
  1.3 25.2 %copy-start.3 = (f32[4]{0:T(128)S(1)}, f32[4]{0:T(128)}, u32[]{:S(2)}) copy-start(f32[4]{0:T(128)} %param.6) | copy-start | bytes 52
  1.4 8.6 %collective-permute-start = (bf16[2,1,4,128,128]{3,4,2,0,1:T(8,128)(2,1)S(1)}, bf16[2,1,4,128,128]{3,4,2,0,1:T(8,128)(2,1)S(1)}, u32[]{:S(2)}, u32[]{:S(2)}) collective-permute-start(bf16[2,1,4,128,128]{3,4,2,0,1:T(8,128)(2,1)S(1)} %get-tuple-element.9), channel_id=1, source_target_pairs={{0,2},{2,4},{4,6},{6,8},{8,10},{10,12},{12,14},{14,16},{16,18},{18... | collective-permute-start | bytes 786440 | tf_op jit(solution)/shard_map/ppermute | solution.py:14
  3.3 8.4 %collective-permute-start.1 = (bf16[2,1,4,128,128]{3,4,2,0,1:T(8,128)(2,1)S(1)}, bf16[2,1,4,128,128]{3,4,2,0,1:T(8,128)(2,1)S(1)}, u32[]{:S(2)}, u32[]{:S(2)}) collective-permute-start(bf16[2,1,4,128,128]{3,4,2,0,1:T(8,128)(2,1)S(1)} %get-tuple-element.10), channel_id=1, source_target_pairs={{2,0},{4,2},{6,4},{8,6},{10,8},{12,10},{14,12},{16,14},{18,16},{20... | collective-permute-start | bytes 786440 | tf_op jit(solution)/shard_map/ppermute | solution.py:17
  11.9 25.9 %collective-permute-start.3 = (bf16[8,1,4,128,128]{3,4,2,0,1:T(8,128)(2,1)S(1)}, bf16[8,1,4,128,128]{3,4,2,0,1:T(8,128)(2,1)S(1)}, u32[]{:S(2)}, u32[]{:S(2)}) collective-permute-start(bf16[8,1,4,128,128]{3,4,2,0,1:T(8,128)(2,1)S(1)} %pad_maximum_fusion.1), channel_id=1, source_target_pairs={{1,0},{3,2},{5,4},{7,6},{9,8},{11,10},{13,12},{15,14},{17,16},{19,... | collective-permute-start | bytes 3145736 | tf_op jit(solution)/shard_map/ppermute | solution.py:17
  14.4 27.7 %collective-permute-start.2 = (bf16[8,1,4,128,128]{3,4,2,0,1:T(8,128)(2,1)S(1)}, bf16[8,1,4,128,128]{3,4,2,0,1:T(8,128)(2,1)}, u32[]{:S(2)}, u32[]{:S(2)}) collective-permute-start(bf16[8,1,4,128,128]{3,4,2,0,1:T(8,128)(2,1)S(1)} %pad_maximum_fusion.1), channel_id=1, source_target_pairs={{0,1},{2,3},{4,5},{6,7},{8,9},{10,11},{12,13},{14,15},{16,17},{18,... | collective-permute-start | bytes 3145736 | tf_op jit(solution)/shard_map/ppermute | solution.py:14
  43.5 4.4 %copy-start.1 = (bf16[4,3,1,128,128]{4,3,2,1,0:T(8,128)(2,1)S(1)}, bf16[4,3,1,128,128]{4,3,2,1,0:T(8,128)(2,1)}, u32[]{:S(2)}) copy-start(bf16[4,3,1,128,128]{4,3,2,1,0:T(8,128)(2,1)} %param.7) | copy-start | bytes 1179652
  59.6 3.1 %copy-start = (bf16[4,3,4,128,128]{3,4,2,0,1:T(8,128)(2,1)S(1)}, bf16[4,3,4,128,128]{3,4,2,0,1:T(8,128)(2,1)}, u32[]{:S(2)}) copy-start(bf16[4,3,4,128,128]{3,4,2,0,1:T(8,128)(2,1)} %get-tuple-element.7) | copy-start | bytes 4718596
where the time goes:
time: 78.1 us; the launch traced here: 77.3 us
  matrix products  29.3 us (38%)
  waiting for transfers between devices  13.7 us (18%)
  between operations  12.7 us (16%)
  starting transfers between devices  10.3 us (13%)
  other arithmetic  8.62 us (11%)
  local copies, waits for them, and re-layouts  2.65 us (3%)
    dot_general x12, matrix products, self_energy(): jnp.einsum('escad,sfd->escaf', left, block, preferred_element_type=jnp.fl...  29.3 us
    ppermute x2, waiting for transfers between devices, padded(): lax.ppermute(lax.slice_in_dim(block, 0, width, axis=dim), axis, backward)  7.28 us
    ppermute x2, starting transfers between devices, padded(): lax.ppermute(lax.slice_in_dim(block, 0, width, axis=dim), axis, backward)  7.05 us
    ppermute x2, waiting for transfers between devices, padded(): lax.ppermute(lax.slice_in_dim(block, block.shape[dim] - width, None, axis...  6.38 us
    convert_element_type x1, other arithmetic, self_energy(): (lower * below.astype(jnp.float32) + upper * above.astype(jnp.float32)).a...  4.37 us
    ppermute x2, starting transfers between devices, padded(): lax.ppermute(lax.slice_in_dim(block, block.shape[dim] - width, None, axis...  3.21 us
    another operation x4, other arithmetic, self_energy(): jnp.stack([occupied, occupied, occupied + 1.0, occupied + 1.0])  2.68 us
    concatenate x2, other arithmetic, padded(): block = jnp.concatenate([low, block, high], axis=dim)  1.57 us
  transfers between devices with their start and end apart: 4, of which 4 were waited for; matrix products, arithmetic and copies ran while one was open for 5% of the time, Pallas kernels for 0%

commit v1 on v0

v1 whole, which is shorter than its diff:
```python
import functools
import jax
import jax.numpy as jnp
from jax import lax
from jax.experimental import pallas as pl
from jax.experimental.pallas import tpu as pltpu
from jax.sharding import PartitionSpec as P

OFFMAX = 2
MESH = pl.DeviceIdType.MESH


def kernel(n_energy, n_cuts, slots, offsets, occupation, green, coupling, out,
           ext, kbuf, kt, acc, local_sem, k_sem, out_sem,
           own_send, own_recv, x_send, x_recv, relay_send, relay_recv):
    rank = lax.axis_index("energy")
    cut = lax.axis_index("cuts")
    count, parts = ext.shape[2] - 2 * OFFMAX, ext.shape[1]
    branches, width = kbuf.shape[0], kbuf.shape[2]
    reach = OFFMAX
    first = rank % 2
    second = 1 - first

    def at(energy, slice_):
        return {"energy": energy, "cuts": slice_}

    has = (rank > 0, rank < n_energy - 1)
    beside = (jnp.maximum(rank - 1, 0), jnp.minimum(rank + 1, n_energy - 1))
    if slots == 1:
        partners = [(1, 1, 1 - cut, None, 2 - 2 * cut)]
    elif slots == 2:
        partners = [
            (1, 2, jnp.maximum(cut - 1, 0), cut > 0, 0),
            (2, 1, jnp.minimum(cut + 1, n_cuts - 1), cut < n_cuts - 1, 2),
        ]
    else:
        partners = []

    def when(cond, do):
        if cond is None:
            do()
        else:
            pl.when(cond)(do)

    def exists(p):
        return jnp.where(p == 0, rank, n_energy - 1 - rank) > 0

    def toward(p):
        return jnp.clip(rank + 2 * p - 1, 0, n_energy - 1)

    def source(p):
        return (count - reach) * p + reach

    def landing(p):
        return (count + reach) * (1 - p)

    def own_copy(p, c):
        return pltpu.make_async_remote_copy(
            src_ref=ext.at[0, c, pl.ds(source(p), reach)],
            dst_ref=ext.at[0, c, pl.ds(landing(p), reach)],
            send_sem=own_send.at[p, c], recv_sem=own_recv.at[p, c],
            device_id=at(toward(p), cut), device_id_type=MESH)

    def relay_copy(slot, p, c):
        return pltpu.make_async_remote_copy(
            src_ref=ext.at[slot, c, pl.ds(source(p), reach)],
            dst_ref=ext.at[slot, c, pl.ds(landing(p), reach)],
            send_sem=relay_send.at[slot - 1, p, c], recv_sem=relay_recv.at[slot - 1, p, c],
            device_id=at(toward(p), cut), device_id_type=MESH)

    def x_copy(there, partner, p, c):
        return pltpu.make_async_remote_copy(
            src_ref=ext.at[0, c, pl.ds(source(p), reach)],
            dst_ref=ext.at[there, c, pl.ds(source(p), reach)],
            send_sem=x_send.at[there - 1, p, c], recv_sem=x_recv.at[there - 1, p, c],
            device_id=at(rank, partner), device_id_type=MESH)

    barrier = pltpu.get_barrier_semaphore()
    for p in range(2):
        pl.when(has[p])(functools.partial(
            pl.semaphore_signal, barrier, inc=1, device_id=at(beside[p], cut), device_id_type=MESH))
    for here, there, partner, cond, side in partners:
        when(cond, functools.partial(
            pl.semaphore_signal, barrier, inc=1, device_id=at(rank, partner), device_id_type=MESH))

    local = [pltpu.make_async_copy(green.at[:, 0, c], ext.at[0, c, pl.ds(reach, count)], local_sem.at[c])
             for c in range(parts)]
    for c in range(parts):
        local[c].start()
    k_copy = pltpu.make_async_copy(coupling.at[:, :, 0], kbuf, k_sem)
    k_copy.start()

    peers = sum(flag.astype(jnp.int32) for flag in has)
    for here, there, partner, cond, side in partners:
        peers = peers + (1 if cond is None else cond.astype(jnp.int32))
    pl.semaphore_wait(barrier, peers)

    order = [(0, 0)]
    for c in range(1, parts):
        order += [(0, c), (1, c - 1)]
    order += [(1, parts - 1)]
    waited = set()
    for which, c in order:
        if c not in waited:
            local[c].wait()
            waited.add(c)
        p = (first, second)[which]
        for here, there, partner, cond, side in partners:
            when(cond, lambda: x_copy(there, partner, p, c).start())
        if which == 0 and c < 2:
            for q in (first, second):
                pl.when(exists(q))(lambda: own_copy(q, c).start())

    @pl.when(rank == 0)
    def _():
        ext[:, :, pl.ds(0, reach)] = jnp.zeros((slots + 1, parts, reach, width, width), ext.dtype)

    @pl.when(rank == n_energy - 1)
    def _():
        ext[:, :, pl.ds(count + reach, reach)] = jnp.zeros((slots + 1, parts, reach, width, width), ext.dtype)

    k_copy.wait()
    for s in range(kbuf.shape[1]):
        for b in range(branches):
            kt[s, b * width:(b + 1) * width, :] = kbuf[b, s].T

    def forward(which, c):
        p = (first, second)[which]
        for here, there, partner, cond, side in partners:
            def go():
                x_copy(here, partner, p, c).wait_recv()
                pl.when(exists(p))(lambda: relay_copy(here, p, c).start())
            when(cond, go)

    def send_own(c):
        for q in (first, second):
            pl.when(exists(q))(lambda: own_copy(q, c).start())

    def own_ready(c):
        for p in range(2):
            pl.when(has[p])(lambda: own_copy(1 - p, c).wait_recv())

    steps = parts * (slots + 1)
    plan = {}
    position = 0
    for k in range(parts):
        todo = []
        if position < len(order):
            todo.append(order[position])
            position += 1
        plan[k] = todo
    k = parts
    if partners:
        plan[k] = [order[position]] if position < len(order) else []
        position += 1
        while position < len(order):
            k = min(k + 1, 2 * parts - 1)
            take = 2 if len(order) - position > 1 else 1
            plan.setdefault(k, [])
            plan[k] += order[position:position + take]
            position += take

    def compute(slot, side, c):
        values = [ext[slot, c, e].astype(jnp.float32) for e in range(count + 2 * reach)]
        lefts = []
        for b in range(branches):
            n = occupation[b]
            w = offsets[b]
            lesser = c < parts // 2
            lower = jnp.where(lesser, n, n + 1.0)
            upper = jnp.where(lesser, n + 1.0, n)
            low = [jnp.where(w == d, lower, 0.0) for d in range(1, reach + 1)]
            up = [jnp.where(w == d, upper, 0.0) for d in range(1, reach + 1)]
            mixed = []
            for e in range(count):
                total = None
                for d in range(1, reach + 1):
                    term = low[d - 1] * values[reach + e - d] + up[d - 1] * values[reach + e + d]
                    total = term if total is None else total + term
                mixed.append(total.astype(jnp.bfloat16))
            lefts.append(jnp.dot(kbuf[b, side], jnp.concatenate(mixed, axis=1),
                                 preferred_element_type=jnp.float32).astype(jnp.bfloat16))
        rows = [jnp.concatenate([left[:, e * width:(e + 1) * width] for left in lefts], axis=1)
                for e in range(count)]
        return jnp.dot(jnp.concatenate(rows, axis=0), kt[side], preferred_element_type=jnp.float32)

    def out_copy(c):
        return pltpu.make_async_copy(acc.at[c], out.at[:, 0, c], out_sem.at[c])

    def step(t, carry):
        slot = t // parts
        c = t % parts
        for k, todo in plan.items():
            if todo or k + 2 < parts:
                @pl.when(t == k)
                def _():
                    for which, part in todo:
                        forward(which, part)
                    if k + 2 < parts:
                        send_own(k + 2)

        @pl.when(slot == 0)
        def _():
            own_ready(c)

        runs = slot == 0
        side = jnp.where(slot == 0, 1, 0)
        for here, there, partner, cond, which_side in partners:
            side = jnp.where(slot == here, which_side, side)
            mine = slot == here
            if cond is not None:
                mine = jnp.logical_and(mine, cond)
            runs = jnp.logical_or(runs, mine)

            @pl.when(mine)
            def _():
                for p in range(2):
                    pl.when(has[p])(lambda: relay_copy(here, 1 - p, c).wait_recv())

        def work():
            sums = compute(slot, side, c)

            @pl.when(slot == 0)
            def _():
                for e in range(count):
                    acc[c, e] = sums[e * width:(e + 1) * width]

            @pl.when(slot > 0)
            def _():
                for e in range(count):
                    acc[c, e] += sums[e * width:(e + 1) * width]

        if slots == 2:
            pl.when(runs)(work)
        else:
            work()

        @pl.when(slot == slots)
        def _():
            out_copy(c).start()
        return carry

    lax.fori_loop(0, steps, step, 0)

    for c in range(parts):
        for p in range(2):
            pl.when(has[p])(lambda: own_copy(p, c).wait_send())
            for here, there, partner, cond, side in partners:
                when(cond, lambda: x_copy(there, partner, p, c).wait_send())
                both = has[p] if cond is None else jnp.logical_and(cond, has[p])
                pl.when(both)(lambda: relay_copy(here, p, c).wait_send())
    for c in range(parts):
        out_copy(c).wait()


def body(n_energy, n_cuts, green, offsets, occupation, coupling):
    count, slices, parts, width, _ = green.shape
    branches, sides = coupling.shape[:2]
    assert slices == 1 and count == 2 * OFFMAX
    slots = min(n_cuts - 1, 2)
    sems = max(slots, 1)
    dma = pltpu.SemaphoreType.DMA
    return pl.pallas_call(
        functools.partial(kernel, n_energy, n_cuts, slots),
        out_shape=jax.ShapeDtypeStruct(green.shape, jnp.float32),
        in_specs=[
            pl.BlockSpec(memory_space=pltpu.SMEM),
            pl.BlockSpec(memory_space=pltpu.SMEM),
            pl.BlockSpec(memory_space=pl.ANY),
            pl.BlockSpec(memory_space=pl.ANY),
        ],
        out_specs=pl.BlockSpec(memory_space=pl.ANY),
        scratch_shapes=[
            pltpu.VMEM((slots + 1, parts, count + 2 * OFFMAX, width, width), jnp.bfloat16),
            pltpu.VMEM((branches, sides, width, width), jnp.bfloat16),
            pltpu.VMEM((sides, branches * width, width), jnp.bfloat16),
            pltpu.VMEM((parts, count, width, width), jnp.float32),
            dma((parts,)),
            dma,
            dma((parts,)),
            dma((2, parts)),
            dma((2, parts)),
            dma((sems, 2, parts)),
            dma((sems, 2, parts)),
            dma((sems, 2, parts)),
            dma((sems, 2, parts)),
        ],
        compiler_params=pltpu.CompilerParams(collective_id=0, has_side_effects=True),
    )(offsets, occupation, green, coupling)


def solution(mesh):
    sizes = dict(mesh.shape)
    in_specs = (P("energy", "cuts", None, None, None), P(), P(), P(None, None, "cuts", None, None))
    out_specs = P("energy", "cuts", None, None, None)
    return jax.shard_map(
        functools.partial(body, sizes["energy"], sizes["cuts"]),
        mesh=mesh, in_specs=in_specs, out_specs=out_specs, check_vma=False)
```

time: 78.1 us -> 23.5 us (0.30)
  the two profiles are of different devices: /device:TPU:26 before, /device:TPU:1 now
where the time goes in v1:
time: 23.5 us; the launch traced here: 23.4 us
  Pallas kernels  21.1 us (90%)
  local copies, waits for them, and re-layouts  2.3 us (10%)
    pallas_call x1, Pallas kernels, body(): pl.pallas_call(functools.partial(kernel, n_energy, n_cuts, slots), out_sh...  21.1 us
    unnamed x1, local copies, waits for them, and re-layouts  2.3 us

profile of v1, /device:TPU:1, one launch (start us, length us, event | category | flops | bytes accessed | tf_op | source)
XLA Modules:
  0.0 23.4 jit_solution(4377570849905658161)
XLA Ops:
  0.0 21.1 %shard_map.46 = f32[4,1,4,128,128]{4,3,2,1,0:T(8,128)} custom-call(s32[4]{0:T(128)} %offsets.1, f32[4]{0:T(128)} %occupation.1, bf16[4,1,4,128,128]{4,3,2,1,0:T(8,128)(2,1)} %green.1, bf16[4,3,1,128,128]{4,3,2,1,0:T(8,128)(2,1)} %coupling.1), custom_call_target="tpu_custom_call" | custom-call | tf_op jit(solution)/shard_map/pallas_call | solution.py:263
  21.1 2.3 %copy.6 = f32[4,1,4,128,128]{4,3,2,1,0:T(8,128)} copy(f32[4,1,4,128,128]{4,3,2,1,0:T(8,128)} %shard_map.46) | data formatting | bytes 2097152

commit v2 on v1

--- a/solution.py
+++ b/solution.py
@@ -10,8 +10,8 @@
 MESH = pl.DeviceIdType.MESH
 
 
-def kernel(n_energy, n_cuts, slots, offsets, occupation, green, coupling, out,
-           ext, kbuf, kt, acc, local_sem, k_sem, out_sem,
+def kernel(n_energy, n_cuts, slots, offsets, occupation, green, coupling, acc,
+           ext, kbuf, kt, local_sem, k_sem,
            own_send, own_recv, x_send, x_recv, relay_send, relay_recv):
     rank = lax.axis_index("energy")
     cut = lax.axis_index("cuts")
@@ -184,9 +184,6 @@
                 for e in range(count)]
         return jnp.dot(jnp.concatenate(rows, axis=0), kt[side], preferred_element_type=jnp.float32)
 
-    def out_copy(c):
-        return pltpu.make_async_copy(acc.at[c], out.at[:, 0, c], out_sem.at[c])
-
     def step(t, carry):
         slot = t // parts
         c = t % parts
@@ -235,9 +232,6 @@
         else:
             work()
 
-        @pl.when(slot == slots)
-        def _():
-            out_copy(c).start()
         return carry
 
     lax.fori_loop(0, steps, step, 0)
@@ -249,8 +243,14 @@
                 when(cond, lambda: x_copy(there, partner, p, c).wait_send())
                 both = has[p] if cond is None else jnp.logical_and(cond, has[p])
                 pl.when(both)(lambda: relay_copy(here, p, c).wait_send())
-    for c in range(parts):
-        out_copy(c).wait()
+
+
+def write_out(sums, out, sem):
+    copies = [pltpu.make_async_copy(sums.at[c], out.at[:, 0, c], sem.at[c]) for c in range(sums.shape[0])]
+    for copy in copies:
+        copy.start()
+    for copy in copies:
+        copy.wait()
 
 
 def body(n_energy, n_cuts, green, offsets, occupation, coupling):
@@ -260,24 +260,22 @@
     slots = min(n_cuts - 1, 2)
     sems = max(slots, 1)
     dma = pltpu.SemaphoreType.DMA
-    return pl.pallas_call(
+    sums = pl.pallas_call(
         functools.partial(kernel, n_energy, n_cuts, slots),
-        out_shape=jax.ShapeDtypeStruct(green.shape, jnp.float32),
+        out_shape=pltpu.VMEM((parts, count, width, width), jnp.float32),
         in_specs=[
             pl.BlockSpec(memory_space=pltpu.SMEM),
             pl.BlockSpec(memory_space=pltpu.SMEM),
             pl.BlockSpec(memory_space=pl.ANY),
             pl.BlockSpec(memory_space=pl.ANY),
         ],
-        out_specs=pl.BlockSpec(memory_space=pl.ANY),
+        out_specs=pl.BlockSpec(memory_space=pltpu.VMEM),
         scratch_shapes=[
             pltpu.VMEM((slots + 1, parts, count + 2 * OFFMAX, width, width), jnp.bfloat16),
             pltpu.VMEM((branches, sides, width, width), jnp.bfloat16),
             pltpu.VMEM((sides, branches * width, width), jnp.bfloat16),
-            pltpu.VMEM((parts, count, width, width), jnp.float32),
             dma((parts,)),
             dma,
-            dma((parts,)),
             dma((2, parts)),
             dma((2, parts)),
             dma((sems, 2, parts)),
@@ -287,6 +285,13 @@
         ],
         compiler_params=pltpu.CompilerParams(collective_id=0, has_side_effects=True),
     )(offsets, occupation, green, coupling)
+    return pl.pallas_call(
+        write_out,
+        out_shape=jax.ShapeDtypeStruct(green.shape, jnp.float32),
+        in_specs=[pl.BlockSpec(memory_space=pltpu.VMEM)],
+        out_specs=pl.BlockSpec(memory_space=pl.ANY),
+        scratch_shapes=[dma((parts,))],
+    )(pltpu.with_memory_space_constraint(sums, pltpu.VMEM))
 
 
 def solution(mesh):

time: 23.5 us -> 21.5 us (0.915)
  local copies, waits for them, and re-layouts: 2.3 us -> 0 us
  Pallas kernels: 21.1 us -> 21.4 us
    unnamed x1 -> x0, local copies, waits for them, and re-layouts: 2.3 us -> none
    pallas_call x0 -> x1, Pallas kernels: none -> 1 us  [body(): pl.pallas_call(write_out, out_shape=jax.ShapeDtypeStruct(green.shape, jnp...]
    pallas_call x1, Pallas kernels: 21.1 us -> 20.4 us  [body(): pl.pallas_call(functools.partial(kernel, n_energy, n_cuts, slots), out_sh...]
where the time goes in v2:
time: 21.5 us; the launch traced here: 21.4 us
  Pallas kernels  21.4 us (100%)
    pallas_call x1, Pallas kernels, body(): pl.pallas_call(functools.partial(kernel, n_energy, n_cuts, slots), out_sh...  20.4 us
    pallas_call x1, Pallas kernels, body(): pl.pallas_call(write_out, out_shape=jax.ShapeDtypeStruct(green.shape, jnp...  1 us

profile of v2, /device:TPU:1, one launch (start us, length us, event | category | flops | bytes accessed | tf_op | source)
XLA Modules:
  0.0 21.4 jit_solution(6073354815978571977)
XLA Ops:
  0.0 20.4 %shard_map.46.sums = f32[4,4,128,128]{3,2,1,0:T(8,128)S(1)} custom-call(s32[4]{0:T(128)} %offsets.1, f32[4]{0:T(128)} %occupation.1, bf16[4,1,4,128,128]{4,3,2,1,0:T(8,128)(2,1)} %green.1, bf16[4,3,1,128,128]{4,3,2,1,0:T(8,128)(2,1)} %coupling.1), custom_call_target="tpu_custom_call" | custom-call | tf_op jit(solution)/shard_map/pallas_call | solution.py:263
  20.4 1.0 %shard_map.47 = f32[4,1,4,128,128]{4,3,2,1,0:T(8,128)} custom-call(f32[4,4,128,128]{3,2,1,0:T(8,128)S(1)} %shard_map.46.sums), custom_call_target="tpu_custom_call" | custom-call | tf_op jit(solution)/shard_map/pallas_call | solution.py:288

commit v3 on v2

--- a/solution.py
+++ b/solution.py
@@ -10,8 +10,8 @@
 MESH = pl.DeviceIdType.MESH
 
 
-def kernel(n_energy, n_cuts, slots, offsets, occupation, green, coupling, acc,
-           ext, kbuf, kt, local_sem, k_sem,
+def kernel(n_energy, n_cuts, slots, offsets_in, occupation_in, green, coupling, acc,
+           offsets, occupation, ext, kbuf, kt, small_sem, local_sem, k_sem,
            own_send, own_recv, x_send, x_recv, relay_send, relay_recv):
     rank = lax.axis_index("energy")
     cut = lax.axis_index("cuts")
@@ -89,6 +89,10 @@
         local[c].start()
     k_copy = pltpu.make_async_copy(coupling.at[:, :, 0], kbuf, k_sem)
     k_copy.start()
+    small = [pltpu.make_async_copy(offsets_in, offsets, small_sem.at[0]),
+             pltpu.make_async_copy(occupation_in, occupation, small_sem.at[1])]
+    for copy in small:
+        copy.start()
 
     peers = sum(flag.astype(jnp.int32) for flag in has)
     for here, there, partner, cond, side in partners:
@@ -107,7 +111,7 @@
         p = (first, second)[which]
         for here, there, partner, cond, side in partners:
             when(cond, lambda: x_copy(there, partner, p, c).start())
-        if which == 0 and c < 2:
+        if which == 0:
             for q in (first, second):
                 pl.when(exists(q))(lambda: own_copy(q, c).start())
 
@@ -120,6 +124,8 @@
         ext[:, :, pl.ds(count + reach, reach)] = jnp.zeros((slots + 1, parts, reach, width, width), ext.dtype)
 
     k_copy.wait()
+    for copy in small:
+        copy.wait()
     for s in range(kbuf.shape[1]):
         for b in range(branches):
             kt[s, b * width:(b + 1) * width, :] = kbuf[b, s].T
@@ -132,33 +138,15 @@
                 pl.when(exists(p))(lambda: relay_copy(here, p, c).start())
             when(cond, go)
 
-    def send_own(c):
-        for q in (first, second):
-            pl.when(exists(q))(lambda: own_copy(q, c).start())
-
     def own_ready(c):
         for p in range(2):
             pl.when(has[p])(lambda: own_copy(1 - p, c).wait_recv())
 
     steps = parts * (slots + 1)
+    last = 2 * parts - 2
     plan = {}
-    position = 0
-    for k in range(parts):
-        todo = []
-        if position < len(order):
-            todo.append(order[position])
-            position += 1
-        plan[k] = todo
-    k = parts
-    if partners:
-        plan[k] = [order[position]] if position < len(order) else []
-        position += 1
-        while position < len(order):
-            k = min(k + 1, 2 * parts - 1)
-            take = 2 if len(order) - position > 1 else 1
-            plan.setdefault(k, [])
-            plan[k] += order[position:position + take]
-            position += take
+    for position, item in enumerate(order if partners else []):
+        plan.setdefault(min(position, last), []).append(item)
 
     def compute(slot, side, c):
         values = [ext[slot, c, e].astype(jnp.float32) for e in range(count + 2 * reach)]
@@ -188,13 +176,10 @@
         slot = t // parts
         c = t % parts
         for k, todo in plan.items():
-            if todo or k + 2 < parts:
-                @pl.when(t == k)
-                def _():
-                    for which, part in todo:
-                        forward(which, part)
-                    if k + 2 < parts:
-                        send_own(k + 2)
+            @pl.when(t == k)
+            def _():
+                for which, part in todo:
+                    forward(which, part)
 
         @pl.when(slot == 0)
         def _():
@@ -264,16 +249,19 @@
         functools.partial(kernel, n_energy, n_cuts, slots),
         out_shape=pltpu.VMEM((parts, count, width, width), jnp.float32),
         in_specs=[
-            pl.BlockSpec(memory_space=pltpu.SMEM),
-            pl.BlockSpec(memory_space=pltpu.SMEM),
+            pl.BlockSpec(memory_space=pl.ANY),
+            pl.BlockSpec(memory_space=pl.ANY),
             pl.BlockSpec(memory_space=pl.ANY),
             pl.BlockSpec(memory_space=pl.ANY),
         ],
         out_specs=pl.BlockSpec(memory_space=pltpu.VMEM),
         scratch_shapes=[
+            pltpu.SMEM(offsets.shape, offsets.dtype),
+            pltpu.SMEM(occupation.shape, occupation.dtype),
             pltpu.VMEM((slots + 1, parts, count + 2 * OFFMAX, width, width), jnp.bfloat16),
             pltpu.VMEM((branches, sides, width, width), jnp.bfloat16),
             pltpu.VMEM((sides, branches * width, width), jnp.bfloat16),
+            dma((2,)),
             dma((parts,)),
             dma,
             dma((2, parts)),

time: 21.5 us -> 19.8 us (0.921)
  Pallas kernels: 21.4 us -> 19.5 us
    pallas_call x1, Pallas kernels: 20.4 us -> 18.5 us  [body(): pl.pallas_call(functools.partial(kernel, n_energy, n_cuts, slots), out_sh...]
where the time goes in v3:
time: 19.8 us; the launch traced here: 19.5 us
  Pallas kernels  19.5 us (98%)
    pallas_call x1, Pallas kernels, body(): pl.pallas_call(functools.partial(kernel, n_energy, n_cuts, slots), out_sh...  18.5 us
    pallas_call x1, Pallas kernels, body(): pl.pallas_call(write_out, out_shape=jax.ShapeDtypeStruct(green.shape, jnp...  1 us

profile of v3, /device:TPU:1, one launch (start us, length us, event | category | flops | bytes accessed | tf_op | source)
XLA Modules:
  0.0 19.5 jit_solution(7422022101305235997)
XLA Ops:
  0.0 18.5 %shard_map.46.sums = f32[4,4,128,128]{3,2,1,0:T(8,128)S(1)} custom-call(s32[4]{0:T(128)} %offsets_in.1, f32[4]{0:T(128)} %occupation_in.1, bf16[4,1,4,128,128]{4,3,2,1,0:T(8,128)(2,1)} %green.1, bf16[4,3,1,128,128]{4,3,2,1,0:T(8,128)(2,1)} %coupling.1), custom_call_target="tpu_custom_call" | custom-call | tf_op jit(solution)/shard_map/pallas_call | solution.py:248
  18.5 1.0 %shard_map.47 = f32[4,1,4,128,128]{4,3,2,1,0:T(8,128)} custom-call(f32[4,4,128,128]{3,2,1,0:T(8,128)S(1)} %shard_map.46.sums), custom_call_target="tpu_custom_call" | custom-call | tf_op jit(solution)/shard_map/pallas_call | solution.py:276
